TPU v7x, 32 devices: a whole 2x2x4 slice. The times are simulated.
32 devices in a mesh: band: 4 (over y, core), col: 8 (over z, x).
Axes of the slice: x: 2, y: 2, z: 4, core: 2. Of those that a mesh axis runs over, the one named last changes fastest.
Arguments:
- source: bfloat16 [6, 524288], P(None, ('band', 'col')), may hold values from -6 to 6
- weights: bfloat16 [8192, 128, 128], P(('band', 'col')), may hold values from -0.5 to 0.5
- source_block: int32 [8192], P(('band', 'col')), may hold values from 0 to 127
- owner_device: int32 [8192, 1], P(('band', 'col')), may hold values from 0 to 31, as said below
- target_tile: int32 [8192], P(('band', 'col')), may hold values from 0 to 112, as said below
- cutoff: int32 [64], P(('band', 'col')), may hold values from 1 to 511
Outputs:
- remapped: float32 [6, 64, 7200], P(None, 'band', 'col')
- filtered: float32 [6, 64, 7200], P(None, 'band', 'col')
Inputs may be any that keep to these rules, and one draw needn't show every extreme that they name: `owner_device`: owners are numbered band index times 8 plus col index. A device's blocks go only to owners in its own band or in the bands next to it. Among the 256 blocks of one device at most 24 share an owner; in every device exactly 24 do for some owner of its own band, and exactly 24 for some owner of each band next to its own; every device sends at least 15 blocks to each owner of its own band. `target_tile`: every tile of every owner receives at least one block.
All inputs are finite; a program needn't handle non-finite values.
Results may differ from a plain program's by a relative error of at most 0.0003.
Values sent between devices are 32-bit elements; how exact they have to be, the bound alone decides.
A program may use at most 64 MiB of HBM per device.

v0:
```python
import functools

import jax
import jax.numpy as jnp
import numpy as np
from jax import lax
from jax.experimental import pallas as pl
from jax.experimental.pallas import tpu as pltpu
from jax.sharding import PartitionSpec as P

NLON = 7200
KW = 512
LANES = 128
STEP = 16
MESH = pl.DeviceIdType.MESH
F32 = jnp.float32
BF16 = jnp.bfloat16


def round_up(value, multiple):
    return (value + multiple - 1) // multiple * multiple


def split(value):
    high = value.astype(BF16)
    return high, (value - high.astype(F32)).astype(BF16)


def dot(left, right, left_dim=1, right_dim=0):
    return lax.dot_general(
        left, right, (((left_dim,), (right_dim,)), ((), ())), preferred_element_type=F32
    )


def remap_kernel(
    bands, cols, levels, capacity, wave_count, period, longitudes, tile_count,
    cutoff, partial, owner_row, tile_row, fine, coarse, start,
    remapped, filtered,
    sums, table_high, table_low, rotated, field, slab, recv, relay, relay_sums, passed,
    spectra, arrived, scaled, gathered,
    send_sem, recv_sem, relay_sem, pass_send, pass_recv,
    scatter_send, scatter_recv, spread_send, spread_recv,
):
    band, col = lax.axis_index("band"), lax.axis_index("col")
    blocks = partial.shape[0]
    rows = levels * capacity
    owners = owner_row[...]
    sublane = lax.broadcasted_iota(jnp.int32, (blocks, blocks), 0)
    lane = lax.broadcasted_iota(jnp.int32, (blocks, blocks), 1)
    owners_wide = jnp.broadcast_to(owners.astype(F32), (8, blocks))
    owner_column = jnp.transpose(owners_wide)[:, 0:1]
    earlier = (owner_column == owners.astype(F32)) & (sublane < lane)
    rank = jnp.sum(earlier.astype(jnp.int32), axis=0, keepdims=True)
    place = owners - (band - 1) * cols
    slot = place * capacity + rank
    data = jnp.concatenate([partial[:, level, :] for level in range(levels)], axis=1)
    stacked = jnp.concatenate(split(data), axis=0)
    slot_lane = lax.broadcasted_iota(jnp.int32, (LANES, blocks), 0)
    tile_at = jnp.where(slot_lane == rank, tile_row[...], 0).astype(F32).astype(BF16)

    def valid(offset):
        target = band + (offset - 1)
        return (target >= 0) & (target < bands)

    def to_others(start_copy):
        def one(step, carry):
            to = lax.rem(col + cols // 2 + step, cols)
            pl.when(to != col)(functools.partial(start_copy, to))
            return carry

        lax.fori_loop(0, cols, one, 0)

    def send(offset):
        group = cols * capacity
        ids = lax.broadcasted_iota(jnp.int32, (group, blocks), 0) + offset * group
        placing = (ids == slot).astype(F32).astype(BF16)
        placed = dot(jnp.concatenate([placing, placing], axis=1), stacked)
        place_ids = lax.broadcasted_iota(jnp.int32, (cols, blocks), 0) + offset * cols
        chosen = (place_ids == place).astype(F32).astype(BF16)
        tags = dot(chosen, tile_at, 1, 1)
        here = pl.ds(offset * cols, cols)
        for level in range(levels):
            piece = placed[:, level * LANES : (level + 1) * LANES]
            slab[here, level * capacity : (level + 1) * capacity, :] = piece.reshape(
                cols, capacity, LANES
            )
        slab[here, rows : rows + 8, :] = jnp.broadcast_to(tags[:, None, :], (cols, 8, LANES))

    half_size = cols // 2
    half, place_in_half = col // half_size, lax.rem(col, half_size)

    def push(owner_half, into, sems, offset):
        def one(step, carry):
            to = lax.rem(place_in_half + half_size // 2 + step, half_size)
            source = slab.at[offset * cols + owner_half * half_size + to]
            target = into.at[(2 - offset) * half_size + place_in_half]

            def start_remote():
                pltpu.make_async_remote_copy(
                    src_ref=source,
                    dst_ref=target,
                    send_sem=send_sem.at[offset],
                    recv_sem=sems.at[2 - offset],
                    device_id=(band + (offset - 1), half * half_size + to),
                    device_id_type=MESH,
                ).start()

            if offset == 1:
                pl.when(to != place_in_half)(start_remote)
            else:
                start_remote()
            return carry

        lax.fori_loop(0, half_size, one, 0)
        if offset == 1:
            pltpu.make_async_copy(
                slab.at[cols + owner_half * half_size + place_in_half],
                into.at[half_size + place_in_half],
                sems.at[1],
            ).start()

    def place_and_push(offset):
        send(offset)
        push(1 - half, relay, relay_sem, offset)

    for offset in (0, 2, 1):
        pl.when(valid(offset))(functools.partial(place_and_push, offset))
    for offset in (0, 2, 1):
        pl.when(valid(offset))(functools.partial(push, half, recv, recv_sem, offset))

    begin = start[col]
    cos_start, sin_start = begin[0:1], begin[1:2]
    rotated[0] = fine[0] * cos_start - fine[1] * sin_start
    rotated[1] = fine[1] * cos_start + fine[0] * sin_start

    def table_step(step, carry):
        pair = coarse[step]
        cos_base, sin_base = pair[0:1], pair[1:2]
        cos_fine, sin_fine = rotated[0], rotated[1]
        at = pl.ds(pl.multiple_of(step * STEP, STEP), STEP)
        for first, value in (
            (0, cos_base * cos_fine - sin_base * sin_fine),
            (wave_count, sin_base * cos_fine + cos_base * sin_fine),
        ):
            high, low = split(value)
            table_high[at, first : first + wave_count] = high
            table_low[at, first : first + wave_count] = low
        return carry

    lax.fori_loop(0, coarse.shape[0], table_step, 0)

    tiles = sums.shape[1]
    sums[...] = jnp.zeros_like(sums)
    relay_sums[...] = jnp.zeros_like(relay_sums)

    def receive(ref, sems, into, offset):
        here = pl.ds(offset * half_size, half_size)
        pltpu.make_async_copy(ref.at[here], ref.at[here], sems.at[offset]).wait()
        tags = jnp.transpose(
            jnp.concatenate([ref[here, rows, :]] * (-(-8 // half_size)), axis=0)
        )
        wide = lax.broadcasted_iota(jnp.int32, (capacity, tiles), 1).astype(F32)
        chooser = jnp.concatenate(
            [
                (tags[:capacity, source : source + 1] == wide).astype(F32)
                for source in range(half_size)
            ],
            axis=0,
        )
        chooser = jnp.transpose(chooser).astype(BF16)
        incoming = jnp.concatenate(
            [
                ref[here, level * capacity : (level + 1) * capacity, :].reshape(
                    half_size * capacity, LANES
                )
                for level in range(levels)
            ],
            axis=1,
        )
        high, low = split(incoming)
        total = dot(chooser, high) + dot(chooser, low)
        for level in range(levels):
            into[level] += total[:, level * LANES : (level + 1) * LANES]

    for offset in (0, 2, 1):
        pl.when(valid(offset))(functools.partial(receive, relay, relay_sem, relay_sums, offset))
    dense = pl.ds(0, tile_count)
    dense_copy = pltpu.make_async_remote_copy(
        src_ref=relay_sums.at[:, dense],
        dst_ref=passed,
        send_sem=pass_send,
        recv_sem=pass_recv,
        device_id=(band, (1 - half) * half_size + place_in_half),
        device_id_type=MESH,
    )
    dense_copy.start()
    for offset in (0, 2, 1):
        pl.when(valid(offset))(functools.partial(receive, recv, recv_sem, sums, offset))
    dense_copy.wait()
    sums[:, :tile_count, :] += passed[...]

    long_tiles, field_rows = field.shape[:2]
    lat_band = field_rows // levels
    shape3 = (levels, long_tiles, LANES)
    lane3 = lax.broadcasted_iota(jnp.int32, shape3, 2)
    inside = lax.broadcasted_iota(jnp.int32, shape3, 1) * LANES + lane3 < longitudes
    for lat in range(lat_band):
        first, shift = divmod(lat * longitudes, LANES)
        value = sums[:, first : first + long_tiles, :]
        if shift:
            after = sums[:, first + 1 : first + 1 + long_tiles, :]
            value = jnp.where(
                lane3 < LANES - shift,
                pltpu.roll(value, LANES - shift, 2),
                pltpu.roll(after, LANES - shift, 2),
            )
        value = jnp.where(inside, value, 0.0)
        for level in range(levels):
            field[:, level * lat_band + lat, :] = value[level]

    rows_wide = jnp.concatenate([field[tile] for tile in range(long_tiles)], axis=1)
    high, low = split(rows_wide)
    both = dot(jnp.concatenate([high, low], axis=0), table_high[...])
    spectrum = both[:field_rows] + both[field_rows:] + dot(high, table_low[...])
    wave_tiles = spectra.shape[2]
    lat_here = lat_band // cols
    for tile in range(wave_tiles):
        spectra[:, :, tile, :] = spectrum[:, tile * LANES : (tile + 1) * LANES].reshape(
            levels, lat_band, LANES
        )

    def lats(ref, index):
        return ref.at[:, pl.ds(index * lat_here, lat_here)]

    def scatter(to):
        pltpu.make_async_remote_copy(
            src_ref=lats(spectra, to),
            dst_ref=arrived.at[col],
            send_sem=scatter_send,
            recv_sem=scatter_recv,
            device_id=(band, to),
            device_id_type=MESH,
        ).start()

    to_others(scatter)
    pltpu.make_async_copy(lats(spectra, col), arrived.at[col], scatter_recv).start()
    remapped[...] = rows_wide[:, :longitudes].reshape(levels, lat_band, longitudes)
    j = (
        lax.broadcasted_iota(jnp.int32, (wave_tiles, LANES), 0) * LANES
        + lax.broadcasted_iota(jnp.int32, (wave_tiles, LANES), 1)
    )
    wave = jnp.where(j >= wave_count, j - wave_count, j)
    weight = jnp.where(wave == 0, 1.0, 2.0) / period
    gains = [jnp.where(wave <= cutoff[lat], weight, 0.0).astype(F32) for lat in range(lat_here)]
    pltpu.make_async_copy(arrived, arrived, scatter_recv).wait()
    for level in range(levels):
        for lat in range(lat_here):
            total = arrived[0, level, lat]
            for source in range(1, cols):
                total += arrived[source, level, lat]
            scaled[level, lat] = total * gains[lat]

    def spread(to):
        pltpu.make_async_remote_copy(
            src_ref=scaled,
            dst_ref=lats(gathered, col),
            send_sem=spread_send,
            recv_sem=spread_recv,
            device_id=(band, to),
            device_id_type=MESH,
        ).start()

    to_others(spread)
    pltpu.make_async_copy(scaled, lats(gathered, col), spread_recv).start()

    def drain(offset):
        sent = slab.at[pl.ds(0, cols - 2 if offset == 1 else cols)]
        pltpu.make_async_copy(sent, sent, send_sem.at[offset]).wait()

    for offset in range(3):
        pl.when(valid(offset))(functools.partial(drain, offset))
    others = arrived.at[pl.ds(0, cols - 1)]
    pltpu.make_async_copy(others, others, scatter_send).wait()

    pltpu.make_async_copy(spectra, gathered, spread_recv).wait()
    spectrum = jnp.concatenate(
        [gathered[:, :, tile, :].reshape(field_rows, LANES) for tile in range(wave_tiles)], axis=1
    )
    high, low = split(spectrum)
    both = dot(jnp.concatenate([high, low], axis=0), table_high[...], 1, 1)
    result = both[:field_rows] + both[field_rows:] + dot(high, table_low[...], 1, 1)
    filtered[...] = result[:, :longitudes].reshape(levels, lat_band, longitudes)
    pltpu.make_async_copy(others, others, spread_send).wait()


def cos_sin(positions):
    phases = positions[:, None] * np.arange(KW)[None, :] % NLON
    angles = phases * (2 * np.pi / NLON)
    return np.cos(angles).astype(np.float32), np.sin(angles).astype(np.float32)


def local(mesh, source, weights, source_block, owner_device, target_tile, cutoff):
    bands, cols = mesh.shape["band"], mesh.shape["col"]
    levels = source.shape[0]
    block_count, block_width = weights.shape[:2]
    lat_here = cutoff.shape[0]
    lat_band = lat_here * cols
    longitudes = NLON // cols
    cell_count = lat_band * longitudes
    tile_count = (cell_count + block_width - 1) // block_width
    regular = (tile_count + cols - 1) // cols
    capacity = regular + max(1, (block_count - cols * regular + 2 * cols - 1) // (2 * cols))
    capacity = round_up(capacity, 8)
    long_pad = round_up(longitudes, LANES)
    long_tiles = long_pad // LANES
    tiles = round_up(tile_count + long_tiles, LANES)
    fine = np.stack(cos_sin(np.arange(STEP)))
    coarse = np.stack(cos_sin(STEP * np.arange(long_pad // STEP)), axis=1)
    start = np.stack(cos_sin(longitudes * np.arange(cols)), axis=1)

    blocks_here = source.reshape(levels, -1, block_width)
    picked = blocks_here.at[:, source_block.astype(jnp.uint32)].get(mode="promise_in_bounds")
    partial = jnp.einsum("lnb,nbt->nlt", picked, weights, preferred_element_type=F32)
    slab_rows = levels * capacity + 8
    wave_tiles = 2 * KW // LANES
    vmem = pl.BlockSpec(memory_space=pltpu.VMEM)
    shape = jax.ShapeDtypeStruct((levels, lat_band, longitudes), F32)
    return pl.pallas_call(
        functools.partial(remap_kernel, bands, cols, levels, capacity, KW, NLON, longitudes, round_up(tile_count, 8)),
        out_shape=(shape, shape),
        in_specs=[pl.BlockSpec(memory_space=pltpu.SMEM)] + [vmem] * 6,
        out_specs=(vmem, vmem),
        scratch_shapes=[
            pltpu.VMEM((levels, tiles, LANES), F32),
            pltpu.VMEM((long_pad, 2 * KW), BF16),
            pltpu.VMEM((long_pad, 2 * KW), BF16),
            pltpu.VMEM((2, STEP, KW), F32),
            pltpu.VMEM((long_tiles, levels * lat_band, LANES), F32),
            pltpu.VMEM((3 * cols, slab_rows, LANES), F32),
            pltpu.VMEM((3 * cols // 2, slab_rows, LANES), F32),
            pltpu.VMEM((3 * cols // 2, slab_rows, LANES), F32),
            pltpu.VMEM((levels, tiles, LANES), F32),
            pltpu.VMEM((levels, round_up(tile_count, 8), LANES), F32),
            pltpu.VMEM((levels, lat_band, wave_tiles, LANES), F32),
            pltpu.VMEM((cols, levels, lat_here, wave_tiles, LANES), F32),
            pltpu.VMEM((levels, lat_here, wave_tiles, LANES), F32),
            pltpu.VMEM((levels, lat_band, wave_tiles, LANES), F32),
            pltpu.SemaphoreType.DMA((3,)),
            pltpu.SemaphoreType.DMA((3,)),
            pltpu.SemaphoreType.DMA((3,)),
            pltpu.SemaphoreType.DMA,
            pltpu.SemaphoreType.DMA,
            pltpu.SemaphoreType.DMA,
            pltpu.SemaphoreType.DMA,
            pltpu.SemaphoreType.DMA,
            pltpu.SemaphoreType.DMA,
        ],
        compiler_params=pltpu.CompilerParams(has_side_effects=True, vmem_limit_bytes=48 << 20),
    )(
        cutoff,
        partial,
        owner_device.reshape(1, block_count),
        target_tile.reshape(1, block_count),
        fine,
        coarse,
        start,
    )


def solution(mesh):
    in_specs = (
        P(None, ("band", "col")),
        P(("band", "col"), None, None),
        P(("band", "col")),
        P(("band", "col"), None),
        P(("band", "col")),
        P(("band", "col")),
    )
    out_specs = (P(None, "band", "col"), P(None, "band", "col"))
    return jax.shard_map(
        functools.partial(local, mesh),
        mesh=mesh,
        in_specs=in_specs,
        out_specs=out_specs,
        check_vma=False,
    )
```

profile of v0, /device:TPU:25, one launch (start us, length us, event | category | flops | bytes accessed | tf_op | source)
XLA Modules:
  0.0 68.6 jit_solution(8834959884635391369)
XLA Ops:
  0.6 0.0 copy-start
  0.6 0.0 copy-start.3
  0.7 0.0 copy-start.1
  0.7 0.0 copy-start.2
  0.7 0.0 copy-start.6
  0.7 0.0 copy-start.5
  0.7 0.0 copy-start.4
  0.7 0.9 %copy-done = bf16[6,16384]{1,0:T(8,128)(2,1)S(1)} copy-done((bf16[6,16384]{1,0:T(8,128)(2,1)S(1)}, bf16[6,16384]{1,0:T(8,128)(2,1)}, u32[]{:S(2)}) %copy-start) | copy-done | bytes 196632
  1.6 0.7 convert_convert_fusion
  2.3 0.8 %gather_fusion = bf16[256,6,128]{2,1,0:T(8,128)(2,1)S(1)} fusion(bf16[6,128,128]{2,0,1:T(8,128)(2,1)S(1)} %bitcast.7, s32[1024]{0:T(1024)S(1)} %pad_clamp_fusion), kind=kCustom, calls=%fused_computation | custom fusion | bytes 787456 | tf_op jit(solution)/shard_map/gather | solution.py:322
  3.1 4.7 %fusion.partial = f32[256,6,128]{2,1,0:T(8,128)S(1)} fusion(bf16[256,128,128]{2,1,0:T(8,128)(2,1)} %param.10, bf16[256,6,128]{2,1,0:T(8,128)(2,1)S(1)} %gather_fusion), kind=kOutput, calls=%fused_computation.1 | convolution fusion | flops 50331648 | bytes 9568256 | tf_op jit(solution)/shard_map/lnb,nbt->nlt/dot_general | solution.py:323
  7.8 0.0 copy-done.3
  7.8 0.0 copy-done.1
  7.8 0.0 copy-done.2
  7.8 0.0 copy-done.6
  7.8 0.0 copy-done.5
  7.8 0.0 copy-done.4
  7.8 59.3 %shard_map.104 = (f32[6,16,900]{2,1,0:T(8,128)S(1)}, f32[6,16,900]{2,1,0:T(8,128)S(1)}) custom-call(s32[2]{0:T(128)S(1)} %copy-done.6, f32[256,6,128]{2,1,0:T(8,128)S(1)} %fusion.partial, s32[1,256]{1,0:T(1,128)S(1)} %bitcast.8, s32[1,256]{1,0:T(1,128)S(1)} %bitcast.9, f32[2,16,512]{2,1,0:T(8,128)S(1)} %copy-done.2, f32[64,2,512]{2,1,0:T(2,128)S(1)} %copy-done.1, ...), custom_call_target="tpu_custom_call" | custom-call | tf_op jit(solution)/shard_map/pallas_call | solution.py:328
  67.1 0.7 %copy.13 = f32[6,16,900]{2,1,0:T(8,128)} copy(f32[6,16,900]{2,1,0:T(8,128)S(1)} %get-tuple-element.4) | data formatting | bytes 691200
  67.8 0.7 %copy.14 = f32[6,16,900]{2,1,0:T(8,128)} copy(f32[6,16,900]{2,1,0:T(8,128)S(1)} %get-tuple-element.5) | data formatting | bytes 691200
  (1 shorter events, 0.0 us)
Async XLA Ops:
  0.6 1.0 %copy-start = (bf16[6,16384]{1,0:T(8,128)(2,1)S(1)}, bf16[6,16384]{1,0:T(8,128)(2,1)}, u32[]{:S(2)}) copy-start(bf16[6,16384]{1,0:T(8,128)(2,1)} %param.9) | copy-start | bytes 589828
  0.6 7.1 %copy-start.3 = (f32[8,2,512]{2,1,0:T(2,128)S(1)}, f32[8,2,512]{2,1,0:T(2,128)}, u32[]{:S(2)}) copy-start(f32[8,2,512]{2,1,0:T(2,128)} %constant.8.clone.start) | copy-start | bytes 98308
  0.7 7.1 %copy-start.1 = (f32[64,2,512]{2,1,0:T(2,128)S(1)}, f32[64,2,512]{2,1,0:T(2,128)}, u32[]{:S(2)}) copy-start(f32[64,2,512]{2,1,0:T(2,128)} %constant.7.clone.coarse) | copy-start | bytes 786436
  0.7 7.1 %copy-start.2 = (f32[2,16,512]{2,1,0:T(8,128)S(1)}, f32[2,16,512]{2,1,0:T(8,128)}, u32[]{:S(2)}) copy-start(f32[2,16,512]{2,1,0:T(8,128)} %constant.6.clone.fine) | copy-start | bytes 196612
  0.7 7.1 %copy-start.6 = (s32[2]{0:T(128)S(1)}, s32[2]{0:T(128)}, u32[]{:S(2)}) copy-start(s32[2]{0:T(128)} %cutoff.1) | copy-start | bytes 28
  0.7 7.1 %copy-start.5 = (s32[256]{0:T(256)S(1)}, s32[256]{0:T(256)}, u32[]{:S(2)}) copy-start(s32[256]{0:T(256)} %param.13) | copy-start | bytes 3076
  0.7 7.1 %copy-start.4 = (s32[256,1]{0,1:T(1,128)S(1)}, s32[256,1]{0,1:T(1,128)}, u32[]{:S(2)}) copy-start(s32[256,1]{0,1:T(1,128)} %param.12) | copy-start | bytes 3076
where the time goes:
time: 68.8 us; the launch traced here: 68.6 us
  Pallas kernels  59.3 us (86%)
  matrix products  4.66 us (7%)
  local copies, waits for them, and re-layouts  3.24 us (5%)
  between operations  0.73 us (1%)
  other arithmetic  0.69 us (1%)
    pallas_call x1, Pallas kernels, local(): pl.pallas_call(functools.partial(remap_kernel, bands, cols, levels, capac...  59.3 us
    dot_general x1, matrix products, local(): jnp.einsum('lnb,nbt->nlt', picked, weights, preferred_element_type=F32)  4.66 us
    unnamed x16, local copies, waits for them, and re-layouts  2.42 us

commit v1 on v0

v1 whole, which is shorter than its diff:
```python
import functools

import jax
import jax.numpy as jnp
import numpy as np
from jax import lax
from jax.experimental import pallas as pl
from jax.experimental.pallas import tpu as pltpu
from jax.sharding import PartitionSpec as P

NLON = 7200
KW = 512
LANES = 128
STEP = 16
CHUNK = 32
PIECE = 8
MESH = pl.DeviceIdType.MESH
F32 = jnp.float32
BF16 = jnp.bfloat16


def round_up(value, multiple):
    return (value + multiple - 1) // multiple * multiple


def split(value):
    high = value.astype(BF16)
    return high, (value - high.astype(F32)).astype(BF16)


def dot(left, right, left_dim=1, right_dim=0):
    return lax.dot_general(
        left, right, (((left_dim,), (right_dim,)), ((), ())), preferred_element_type=F32
    )


def remap_kernel(
    bands, cols, levels, capacity, wave_count, period, longitudes, tile_count,
    cutoff, source_block, owner_row, tile_row, fine, coarse, start, source, weights,
    remapped, filtered,
    weight_buf, source_buf, source_even, source_odd, partial,
    sums, table_high, table_low, rotated, field, slab, recv, relay, relay_sums, passed,
    tags_out, tags_in, cut_out, cut_in,
    spectra, arrived, half_sum, other_sum, scaled, gathered,
    weight_sem, source_sem, tag_send, tag_recv, cut_send, cut_recv,
    send_sem, recv_sem, relay_sem, pass_send, pass_recv,
    scatter_send, scatter_recv, cross_send, cross_recv, spread_send, spread_recv,
):
    band, col = lax.axis_index("band"), lax.axis_index("col")
    blocks = weights.shape[0]
    rows = levels * capacity
    half_size = cols // 2
    half, place_in_half = col // half_size, lax.rem(col, half_size)
    counterpart = (band, (1 - half) * half_size + place_in_half)

    def valid(offset):
        target = band + (offset - 1)
        return (target >= 0) & (target < bands)

    weight_copies = [
        pltpu.make_async_copy(
            weights.at[pl.ds(first, CHUNK)], weight_buf.at[pl.ds(first, CHUNK)], weight_sem.at[i]
        )
        for i, first in enumerate(range(0, blocks, CHUNK))
    ]
    source_copy = pltpu.make_async_copy(source, source_buf, source_sem)
    source_copy.start()
    for copy in weight_copies:
        copy.start()

    barrier = pltpu.get_barrier_semaphore()

    def greet(device):
        pl.semaphore_signal(barrier, inc=1, device_id=device, device_id_type=MESH)

    def greet_half(offset):
        def one(to, carry):
            def signal():
                greet((band + (offset - 1), half * half_size + to))

            if offset == 1:
                pl.when(to != place_in_half)(signal)
            else:
                signal()
            return carry

        lax.fori_loop(0, half_size, one, 0)

    for offset in (0, 2, 1):
        pl.when(valid(offset))(functools.partial(greet_half, offset))
    greet(counterpart)

    owners = owner_row[...]
    sublane = lax.broadcasted_iota(jnp.int32, (blocks, blocks), 0)
    lane = lax.broadcasted_iota(jnp.int32, (blocks, blocks), 1)
    owners_wide = jnp.broadcast_to(owners.astype(F32), (8, blocks))
    owner_column = jnp.transpose(owners_wide)[:, 0:1]
    earlier = (owner_column == owners.astype(F32)) & (sublane < lane)
    rank = jnp.sum(earlier.astype(jnp.int32), axis=0, keepdims=True)
    place = owners - (band - 1) * cols
    slot = place * capacity + rank
    slot_lane = lax.broadcasted_iota(jnp.int32, (LANES, blocks), 0)
    tile_at = jnp.where(slot_lane == rank, tile_row[...], 0).astype(F32).astype(BF16)
    place_ids = lax.broadcasted_iota(jnp.int32, (3 * cols, blocks), 0)
    chosen = (place_ids == place).astype(F32).astype(BF16)
    tags = dot(chosen, tile_at, 1, 1)
    for offset in range(3):
        for to in range(half_size):
            first = tags[offset * cols + to : offset * cols + to + 1]
            second = tags[offset * cols + half_size + to : offset * cols + half_size + to + 1]
            tags_out[offset * half_size + to, 0:1] = jnp.where(half == 0, first, second)
            tags_out[offset * half_size + to, 1:2] = jnp.where(half == 0, second, first)
    lat_here = cutoff.shape[0]
    for lat in range(lat_here):
        cut_out[lat : lat + 1] = jnp.full((1, LANES), cutoff[lat], jnp.int32)

    source_copy.wait()
    above = jnp.zeros((16 - levels, LANES), BF16)
    below = jnp.zeros((8, LANES), BF16)
    for index in range(source_even.shape[0]):
        value = source_buf[:, index * LANES : (index + 1) * LANES]
        source_even[index] = jnp.concatenate([value, above], axis=0)
        source_odd[index] = jnp.concatenate([below, value, above[: 8 - levels]], axis=0)

    for i, copy in enumerate(weight_copies):
        copy.wait()
        for index in range(i * CHUNK, (i + 1) * CHUNK, 2):
            left = jnp.concatenate(
                [source_even[source_block[index]], source_odd[source_block[index + 1]]], axis=1
            )
            right = weight_buf[index : index + 2].reshape(2 * LANES, LANES)
            partial[index : index + 2] = dot(left, right).reshape(2, 8, LANES)

    inner_band = (band > 0) & (band < bands - 1)
    neighbours = jnp.where(inner_band, 2, 1) if bands > 1 else 0
    pl.semaphore_wait(barrier, half_size * (1 + neighbours))

    def send_to_half(source_of, target, sems_out, sems_in, offset):
        def one(step, carry):
            to = lax.rem(place_in_half + half_size // 2 + step, half_size)

            def start_remote():
                pltpu.make_async_remote_copy(
                    src_ref=source_of(to),
                    dst_ref=target,
                    send_sem=sems_out.at[offset],
                    recv_sem=sems_in.at[2 - offset],
                    device_id=(band + (offset - 1), half * half_size + to),
                    device_id_type=MESH,
                ).start()

            if offset == 1:
                pl.when(to != place_in_half)(start_remote)
            else:
                start_remote()
            return carry

        lax.fori_loop(0, half_size, one, 0)
        if offset == 1:
            pltpu.make_async_copy(source_of(place_in_half), target, sems_in.at[1]).start()

    def push_tags(offset):
        send_to_half(
            lambda to: tags_out.at[offset * half_size + to],
            tags_in.at[(2 - offset) * half_size + place_in_half],
            tag_send, tag_recv, offset,
        )

    def push(owner_half, into, sems, offset):
        send_to_half(
            lambda to: slab.at[offset * cols + owner_half * half_size + to],
            into.at[(2 - offset) * half_size + place_in_half],
            send_sem, sems, offset,
        )

    cut_copy = pltpu.make_async_remote_copy(
        src_ref=cut_out,
        dst_ref=cut_in,
        send_sem=cut_send,
        recv_sem=cut_recv,
        device_id=counterpart,
        device_id_type=MESH,
    )
    for offset in (0, 2, 1):
        pl.when(valid(offset))(functools.partial(push_tags, offset))
    cut_copy.start()

    data = jnp.concatenate([partial[:, level, :] for level in range(levels)], axis=1)
    stacked = jnp.concatenate(split(data), axis=0)

    def fill(offset):
        group = cols * capacity
        ids = lax.broadcasted_iota(jnp.int32, (group, blocks), 0) + offset * group
        placing = (ids == slot).astype(F32).astype(BF16)
        placed = dot(jnp.concatenate([placing, placing], axis=1), stacked)
        here = pl.ds(offset * cols, cols)
        for level in range(levels):
            piece = placed[:, level * LANES : (level + 1) * LANES]
            slab[here, level * capacity : (level + 1) * capacity, :] = piece.reshape(
                cols, capacity, LANES
            )

    def place_and_push(offset):
        fill(offset)
        push(1 - half, relay, relay_sem, offset)

    for offset in (0, 2, 1):
        pl.when(valid(offset))(functools.partial(place_and_push, offset))
    for offset in (0, 2, 1):
        pl.when(valid(offset))(functools.partial(push, half, recv, recv_sem, offset))

    begin = start[col]
    cos_start, sin_start = begin[0:1], begin[1:2]
    rotated[0] = fine[0] * cos_start - fine[1] * sin_start
    rotated[1] = fine[1] * cos_start + fine[0] * sin_start
    parity = wave_count // 2

    def table_step(step, carry):
        pair = coarse[step]
        cos_base, sin_base = pair[0:1], pair[1:2]
        cos_fine, sin_fine = rotated[0], rotated[1]
        at = pl.ds(pl.multiple_of(step * STEP, STEP), STEP)
        for first, value in (
            (0, cos_base * cos_fine - sin_base * sin_fine),
            (parity, sin_base * cos_fine + cos_base * sin_fine),
        ):
            high, low = split(value)
            for odd in range(2):
                here = slice(first + odd * wave_count, first + odd * wave_count + parity)
                there = slice(odd * parity, (odd + 1) * parity)
                table_high[at, here] = high[:, there]
                table_low[at, here] = low[:, there]
        return carry

    lax.fori_loop(0, coarse.shape[0], table_step, 0)

    tiles = sums.shape[1]
    sums[...] = jnp.zeros_like(sums)
    relay_sums[...] = jnp.zeros_like(relay_sums)

    def wait_tags(offset):
        here = tags_in.at[pl.ds(offset * half_size, half_size)]
        pltpu.make_async_copy(here, here, tag_recv.at[offset]).wait()

    for offset in (0, 2, 1):
        pl.when(valid(offset))(functools.partial(wait_tags, offset))

    def receive(ref, sems, into, kind, offset):
        here = pl.ds(offset * half_size, half_size)
        tag_rows = [
            tags_in[offset * half_size + sender, kind : kind + 1] for sender in range(half_size)
        ]
        tags = jnp.transpose(jnp.concatenate(tag_rows * (-(-8 // half_size)), axis=0))
        wide = lax.broadcasted_iota(jnp.int32, (capacity, tiles), 1).astype(F32)
        chooser = jnp.concatenate(
            [
                (tags[:capacity, sender : sender + 1] == wide).astype(F32)
                for sender in range(half_size)
            ],
            axis=0,
        )
        chooser = jnp.transpose(chooser).astype(BF16)
        pltpu.make_async_copy(ref.at[here], ref.at[here], sems.at[offset]).wait()
        incoming = jnp.concatenate(
            [
                ref[here, level * capacity : (level + 1) * capacity, :].reshape(
                    half_size * capacity, LANES
                )
                for level in range(levels)
            ],
            axis=1,
        )
        high, low = split(incoming)
        total = dot(chooser, high) + dot(chooser, low)
        for level in range(levels):
            into[level] += total[:, level * LANES : (level + 1) * LANES]

    def dense_start(first, count):
        here = (pl.ds(first, count), pl.ds(0, tile_count))
        pltpu.make_async_remote_copy(
            src_ref=relay_sums.at[here],
            dst_ref=passed.at[pl.ds(first, count)],
            send_sem=pass_send,
            recv_sem=pass_recv,
            device_id=counterpart,
            device_id_type=MESH,
        ).start()

    outer = (place_in_half < half_size // 2) == (half == 0)
    inner = jnp.logical_not(outer)
    first_part, second_part = levels // 4, levels // 2

    for offset in (0, 2, 1):
        pl.when(valid(offset))(functools.partial(receive, relay, relay_sem, relay_sums, 1, offset))
    pl.when(inner)(functools.partial(dense_start, 0, levels))
    for offset in (0, 2, 1):
        pl.when(valid(offset))(functools.partial(receive, recv, recv_sem, sums, 0, offset))

    long_tiles, field_rows = field.shape[1:3]
    lat_band = field_rows // levels
    group_rows = field_rows // half_size
    shape3 = (levels, long_tiles, LANES)
    lane3 = lax.broadcasted_iota(jnp.int32, shape3, 2)
    inside = lax.broadcasted_iota(jnp.int32, shape3, 1) * LANES + lane3 < longitudes

    def row_of(level, lat):
        owner, within = divmod(lat, lat_here)
        lat_half, owner_place = divmod(owner, half_size)
        return owner_place * group_rows + (level * 2 + lat_half) * lat_here + within

    def lat_rows(ref, lat):
        first, shift = divmod(lat * longitudes, LANES)
        value = ref[:, first : first + long_tiles, :]
        if shift:
            after = ref[:, first + 1 : first + 1 + long_tiles, :]
            value = jnp.where(
                lane3 < LANES - shift,
                pltpu.roll(value, LANES - shift, 2),
                pltpu.roll(after, LANES - shift, 2),
            )
        return jnp.where(inside, value, 0.0)

    for lat in range(lat_band):
        own, relayed = lat_rows(sums, lat), lat_rows(relay_sums, lat)
        both, apart = own + relayed, own - relayed
        for level in range(levels):
            field[0, :, row_of(level, lat), :] = both[level]
            field[1, :, row_of(level, lat), :] = apart[level]

    for odd in range(2):
        rows_wide = jnp.concatenate([field[odd, tile] for tile in range(long_tiles)], axis=1)
        high, low = split(rows_wide)
        waves = slice(odd * wave_count, (odd + 1) * wave_count)
        both = dot(jnp.concatenate([high, low], axis=0), table_high[:, waves])
        spectrum = both[:field_rows] + both[field_rows:] + dot(high, table_low[:, waves])
        spectra[:, :, waves] = spectrum.reshape(half_size, group_rows, wave_count)

    pieces = [pl.ds(first, PIECE) for first in range(0, group_rows, PIECE)]

    def to_half(source_of, target, sem_out, sem_in):
        def one(step, carry):
            to = lax.rem(place_in_half + half_size // 2 + step, half_size)

            def start_remote():
                pltpu.make_async_remote_copy(
                    src_ref=source_of(to),
                    dst_ref=target,
                    send_sem=sem_out,
                    recv_sem=sem_in,
                    device_id=(band, half * half_size + to),
                    device_id_type=MESH,
                ).start()

            pl.when(to != place_in_half)(start_remote)
            return carry

        lax.fori_loop(0, half_size, one, 0)
        pltpu.make_async_copy(source_of(place_in_half), target, sem_in).start()

    for i, piece in enumerate(pieces):
        to_half(
            lambda to: spectra.at[to, piece],
            arrived.at[place_in_half, piece],
            scatter_send.at[i], scatter_recv.at[i],
        )
    pl.when(outer)(functools.partial(dense_start, 0, first_part))

    cut_copy.wait()
    cuts = []
    for lat_half in range(2):
        for lat in range(lat_here):
            cuts.append(
                jnp.where(half == lat_half, cut_out[lat : lat + 1], cut_in[lat : lat + 1])
            )
    cut_rows = jnp.concatenate(cuts * (PIECE // len(cuts)), axis=0)

    def gain_of(tile):
        j = lax.broadcasted_iota(jnp.int32, (PIECE, LANES), 1) + tile * LANES
        odd, within = j // wave_count, lax.rem(j, wave_count)
        wave = 2 * lax.rem(within, parity) + odd
        weight = jnp.where(wave == 0, 1.0, 2.0) / period
        return jnp.where(wave <= cut_rows, weight, 0.0).astype(F32)

    wave_tiles = spectra.shape[2] // LANES
    gains = jnp.concatenate([gain_of(tile) for tile in range(wave_tiles)], axis=1)

    def cross(i):
        return pltpu.make_async_remote_copy(
            src_ref=half_sum.at[pieces[i]],
            dst_ref=other_sum.at[pieces[i]],
            send_sem=cross_send.at[i],
            recv_sem=cross_recv.at[i],
            device_id=counterpart,
            device_id_type=MESH,
        )

    for i, piece in enumerate(pieces):
        here = arrived.at[:, piece]
        pltpu.make_async_copy(here, here, scatter_recv.at[i]).wait()
        total = arrived[0, piece]
        for sender in range(1, half_size):
            total += arrived[sender, piece]
        half_sum[piece] = total
        cross(i).start()
    pl.when(outer)(functools.partial(dense_start, first_part, second_part))
    for i, piece in enumerate(pieces):
        cross(i).wait_recv()
        scaled[piece] = (half_sum[piece] + other_sum[piece]) * gains
        to_half(
            lambda to: scaled.at[piece],
            gathered.at[place_in_half, piece],
            spread_send.at[i], spread_recv.at[i],
        )
    rest = first_part + second_part
    pl.when(outer)(functools.partial(dense_start, rest, levels - rest))

    def drain(offset):
        sent = slab.at[pl.ds(0, cols - 2 if offset == 1 else cols)]
        pltpu.make_async_copy(sent, sent, send_sem.at[offset]).wait()
        tag = tags_out.at[pl.ds(0, half_size - 1 if offset == 1 else half_size)]
        pltpu.make_async_copy(tag, tag, tag_send.at[offset]).wait()

    for offset in range(3):
        pl.when(valid(offset))(functools.partial(drain, offset))
    for i, piece in enumerate(pieces):
        others = arrived.at[pl.ds(0, half_size - 1), piece]
        pltpu.make_async_copy(others, others, scatter_send.at[i]).wait()
        cross(i).wait_send()

    def natural(spread):
        rows_of = [
            spread[row : row + lat_here]
            for level in range(levels)
            for row in (row_of(level, lat) for lat in range(0, lat_band, lat_here))
        ]
        return jnp.concatenate(rows_of, axis=0)[:, :longitudes].reshape(
            levels, lat_band, longitudes
        )

    for i, piece in enumerate(pieces):
        here = gathered.at[:, piece]
        pltpu.make_async_copy(here, here, spread_recv.at[i]).wait()
    spectrum = gathered[...].reshape(field_rows, 2 * wave_count)
    high, low = split(spectrum)
    both = dot(jnp.concatenate([high, low], axis=0), table_high[...], 1, 1)
    result = both[:field_rows] + both[field_rows:] + dot(high, table_low[...], 1, 1)
    filtered[...] = natural(result)

    pltpu.make_async_copy(passed, passed, pass_recv).wait()
    sums[:, :tile_count, :] += passed[...]
    for lat in range(lat_band):
        value = lat_rows(sums, lat)
        for level in range(levels):
            field[0, :, level * lat_band + lat, :] = value[level]
    rows_wide = jnp.concatenate([field[0, tile] for tile in range(long_tiles)], axis=1)
    remapped[...] = rows_wide[:, :longitudes].reshape(levels, lat_band, longitudes)

    pltpu.make_async_copy(passed, passed, pass_send).wait()
    for i, piece in enumerate(pieces):
        others = arrived.at[pl.ds(0, half_size - 1), piece]
        pltpu.make_async_copy(others, others, spread_send.at[i]).wait()


def cos_sin(positions):
    waves = np.concatenate([np.arange(0, KW, 2), np.arange(1, KW, 2)])
    phases = positions[:, None] * waves[None, :] % NLON
    angles = phases * (2 * np.pi / NLON)
    return np.cos(angles).astype(np.float32), np.sin(angles).astype(np.float32)


def local(mesh, source, weights, source_block, owner_device, target_tile, cutoff):
    bands, cols = mesh.shape["band"], mesh.shape["col"]
    levels = source.shape[0]
    block_count, block_width = weights.shape[:2]
    lat_here = cutoff.shape[0]
    lat_band = lat_here * cols
    half_size = cols // 2
    longitudes = NLON // cols
    cell_count = lat_band * longitudes
    tile_count = (cell_count + block_width - 1) // block_width
    regular = (tile_count + cols - 1) // cols
    capacity = regular + max(1, (block_count - cols * regular + 2 * cols - 1) // (2 * cols))
    capacity = round_up(capacity, 8)
    long_pad = round_up(longitudes, LANES)
    long_tiles = long_pad // LANES
    tiles = round_up(tile_count + long_tiles, LANES)
    sent_tiles = round_up(tile_count, 8)
    group_rows = levels * lat_band // half_size
    pieces = group_rows // PIECE
    chunks = block_count // CHUNK
    fine = np.stack(cos_sin(np.arange(STEP)))
    coarse = np.stack(cos_sin(STEP * np.arange(long_pad // STEP)), axis=1)
    start = np.stack(cos_sin(longitudes * np.arange(cols)), axis=1)

    slab_rows = levels * capacity
    smem = pl.BlockSpec(memory_space=pltpu.SMEM)
    vmem = pl.BlockSpec(memory_space=pltpu.VMEM)
    anywhere = pl.BlockSpec(memory_space=pl.ANY)
    shape = jax.ShapeDtypeStruct((levels, lat_band, longitudes), F32)
    dma = pltpu.SemaphoreType.DMA
    return pl.pallas_call(
        functools.partial(
            remap_kernel, bands, cols, levels, capacity, KW, NLON, longitudes, sent_tiles
        ),
        out_shape=(shape, shape),
        in_specs=[smem] * 2 + [vmem] * 5 + [anywhere] * 2,
        out_specs=(vmem, vmem),
        scratch_shapes=[
            pltpu.VMEM(weights.shape, BF16),
            pltpu.VMEM(source.shape, BF16),
            pltpu.VMEM((source.shape[1] // LANES, 16, LANES), BF16),
            pltpu.VMEM((source.shape[1] // LANES, 16, LANES), BF16),
            pltpu.VMEM((block_count, 8, LANES), F32),
            pltpu.VMEM((levels, tiles, LANES), F32),
            pltpu.VMEM((long_pad, 2 * KW), BF16),
            pltpu.VMEM((long_pad, 2 * KW), BF16),
            pltpu.VMEM((2, STEP, KW), F32),
            pltpu.VMEM((2, long_tiles, levels * lat_band, LANES), F32),
            pltpu.VMEM((3 * cols, slab_rows, LANES), F32),
            pltpu.VMEM((3 * half_size, slab_rows, LANES), F32),
            pltpu.VMEM((3 * half_size, slab_rows, LANES), F32),
            pltpu.VMEM((levels, tiles, LANES), F32),
            pltpu.VMEM((levels, sent_tiles, LANES), F32),
            pltpu.VMEM((3 * half_size, 2, LANES), F32),
            pltpu.VMEM((3 * half_size, 2, LANES), F32),
            pltpu.VMEM((lat_here, LANES), jnp.int32),
            pltpu.VMEM((lat_here, LANES), jnp.int32),
            pltpu.VMEM((half_size, group_rows, 2 * KW), F32),
            pltpu.VMEM((half_size, group_rows, 2 * KW), F32),
            pltpu.VMEM((group_rows, 2 * KW), F32),
            pltpu.VMEM((group_rows, 2 * KW), F32),
            pltpu.VMEM((group_rows, 2 * KW), F32),
            pltpu.VMEM((half_size, group_rows, 2 * KW), F32),
            dma((chunks,)),
            dma,
            dma((3,)),
            dma((3,)),
            dma,
            dma,
            dma((3,)),
            dma((3,)),
            dma((3,)),
            dma,
            dma,
            dma((pieces,)),
            dma((pieces,)),
            dma((pieces,)),
            dma((pieces,)),
            dma((pieces,)),
            dma((pieces,)),
        ],
        compiler_params=pltpu.CompilerParams(
            collective_id=0, has_side_effects=True, vmem_limit_bytes=56 << 20
        ),
    )(
        cutoff,
        source_block,
        owner_device.reshape(1, block_count),
        target_tile.reshape(1, block_count),
        fine,
        coarse,
        start,
        source,
        weights,
    )


def solution(mesh):
    in_specs = (
        P(None, ("band", "col")),
        P(("band", "col"), None, None),
        P(("band", "col")),
        P(("band", "col"), None),
        P(("band", "col")),
        P(("band", "col")),
    )
    out_specs = (P(None, "band", "col"), P(None, "band", "col"))
    return jax.shard_map(
        functools.partial(local, mesh),
        mesh=mesh,
        in_specs=in_specs,
        out_specs=out_specs,
        check_vma=False,
    )
```

time: 68.8 us -> 63.8 us (0.927)
  the two profiles are of different devices: /device:TPU:25 before, /device:TPU:12 now
where the time goes in v1:
time: 63.8 us; the launch traced here: 63.6 us
  Pallas kernels  59.4 us (93%)
  local copies, waits for them, and re-layouts  3.53 us (6%)
  between operations  0.64 us (1%)
    pallas_call x1, Pallas kernels, local(): pl.pallas_call(functools.partial(remap_kernel, bands, cols, levels, capac...  59.4 us
    unnamed x2, local copies, waits for them, and re-layouts  3.53 us

profile of v1, /device:TPU:12, one launch (start us, length us, event | category | flops | bytes accessed | tf_op | source)
XLA Modules:
  0.0 63.6 jit_solution(3454473094032511202)
XLA Ops:
  0.6 59.4 %shard_map.104 = (f32[6,16,900]{2,1,0:T(8,128)}, f32[6,16,900]{2,1,0:T(8,128)}) custom-call(s32[2]{0:T(128)} %cutoff.1, s32[256]{0:T(256)} %source_block.1, s32[1,256]{1,0:T(1,128)} %bitcast.2, s32[1,256]{1,0:T(1,128)} %bitcast.3, f32[2,16,512]{2,1,0:T(8,128)} %constant.6.clone.fine, f32[64,2,512]{2,1,0:T(2,128)} %constant.7.clone.coarse, ...), custom_call_target="tpu_custom_call" | custom-call | tf_op jit(solution)/shard_map/pallas_call | solution.py:501
  60.1 1.8 %copy.13 = f32[6,16,900]{2,1,0:T(8,128)} copy(f32[6,16,900]{2,1,0:T(8,128)} %get-tuple-element.4) | data formatting | bytes 691200
  61.9 1.8 %copy.14 = f32[6,16,900]{2,1,0:T(8,128)} copy(f32[6,16,900]{2,1,0:T(8,128)} %get-tuple-element.5) | data formatting | bytes 691200

commit v2 on v1

--- a/solution.py
+++ b/solution.py
@@ -14,6 +14,7 @@
 STEP = 16
 CHUNK = 32
 PIECE = 8
+DENSE = (0, 2, 3, 5, 6)
 MESH = pl.DeviceIdType.MESH
 F32 = jnp.float32
 BF16 = jnp.bfloat16
@@ -38,11 +39,11 @@
     bands, cols, levels, capacity, wave_count, period, longitudes, tile_count,
     cutoff, source_block, owner_row, tile_row, fine, coarse, start, source, weights,
     remapped, filtered,
-    weight_buf, source_buf, source_even, source_odd, partial,
+    weight_buf, source_even, source_odd, partial,
     sums, table_high, table_low, rotated, field, slab, recv, relay, relay_sums, passed,
     tags_out, tags_in, cut_out, cut_in,
     spectra, arrived, half_sum, other_sum, scaled, gathered,
-    weight_sem, source_sem, tag_send, tag_recv, cut_send, cut_recv,
+    weight_sem, tag_send, tag_recv, cut_send, cut_recv,
     send_sem, recv_sem, relay_sem, pass_send, pass_recv,
     scatter_send, scatter_recv, cross_send, cross_recv, spread_send, spread_recv,
 ):
@@ -63,8 +64,6 @@
         )
         for i, first in enumerate(range(0, blocks, CHUNK))
     ]
-    source_copy = pltpu.make_async_copy(source, source_buf, source_sem)
-    source_copy.start()
     for copy in weight_copies:
         copy.start()
 
@@ -114,11 +113,10 @@
     for lat in range(lat_here):
         cut_out[lat : lat + 1] = jnp.full((1, LANES), cutoff[lat], jnp.int32)
 
-    source_copy.wait()
     above = jnp.zeros((16 - levels, LANES), BF16)
     below = jnp.zeros((8, LANES), BF16)
     for index in range(source_even.shape[0]):
-        value = source_buf[:, index * LANES : (index + 1) * LANES]
+        value = source[:, index * LANES : (index + 1) * LANES]
         source_even[index] = jnp.concatenate([value, above], axis=0)
         source_odd[index] = jnp.concatenate([below, value, above[: 8 - levels]], axis=0)
 
@@ -286,13 +284,15 @@
             device_id_type=MESH,
         ).start()
 
-    outer = (place_in_half < half_size // 2) == (half == 0)
-    inner = jnp.logical_not(outer)
-    first_part, second_part = levels // 4, levels // 2
+    ends = [levels * share // DENSE[-1] for share in DENSE]
+
+    def dense_part(index):
+        if ends[index + 1] > ends[index]:
+            dense_start(ends[index], ends[index + 1] - ends[index])
 
     for offset in (0, 2, 1):
         pl.when(valid(offset))(functools.partial(receive, relay, relay_sem, relay_sums, 1, offset))
-    pl.when(inner)(functools.partial(dense_start, 0, levels))
+    dense_part(0)
     for offset in (0, 2, 1):
         pl.when(valid(offset))(functools.partial(receive, recv, recv_sem, sums, 0, offset))
 
@@ -363,7 +363,7 @@
             arrived.at[place_in_half, piece],
             scatter_send.at[i], scatter_recv.at[i],
         )
-    pl.when(outer)(functools.partial(dense_start, 0, first_part))
+    dense_part(1)
 
     cut_copy.wait()
     cuts = []
@@ -402,7 +402,7 @@
             total += arrived[sender, piece]
         half_sum[piece] = total
         cross(i).start()
-    pl.when(outer)(functools.partial(dense_start, first_part, second_part))
+    dense_part(2)
     for i, piece in enumerate(pieces):
         cross(i).wait_recv()
         scaled[piece] = (half_sum[piece] + other_sum[piece]) * gains
@@ -411,8 +411,7 @@
             gathered.at[place_in_half, piece],
             spread_send.at[i], spread_recv.at[i],
         )
-    rest = first_part + second_part
-    pl.when(outer)(functools.partial(dense_start, rest, levels - rest))
+    dense_part(3)
 
     def drain(offset):
         sent = slab.at[pl.ds(0, cols - 2 if offset == 1 else cols)]
@@ -503,11 +502,10 @@
             remap_kernel, bands, cols, levels, capacity, KW, NLON, longitudes, sent_tiles
         ),
         out_shape=(shape, shape),
-        in_specs=[smem] * 2 + [vmem] * 5 + [anywhere] * 2,
+        in_specs=[smem] * 2 + [vmem] * 6 + [anywhere],
         out_specs=(vmem, vmem),
         scratch_shapes=[
             pltpu.VMEM(weights.shape, BF16),
-            pltpu.VMEM(source.shape, BF16),
             pltpu.VMEM((source.shape[1] // LANES, 16, LANES), BF16),
             pltpu.VMEM((source.shape[1] // LANES, 16, LANES), BF16),
             pltpu.VMEM((block_count, 8, LANES), F32),
@@ -532,7 +530,6 @@
             pltpu.VMEM((group_rows, 2 * KW), F32),
             pltpu.VMEM((half_size, group_rows, 2 * KW), F32),
             dma((chunks,)),
-            dma,
             dma((3,)),
             dma((3,)),
             dma,

time: 63.8 us -> 55.1 us (0.86)
  the two profiles are of different devices: /device:TPU:12 before, /device:TPU:1 now
where the time goes in v2:
time: 55.1 us; the launch traced here: 54.9 us
  Pallas kernels  50.7 us (92%)
  local copies, waits for them, and re-layouts  3.53 us (6%)
  between operations  0.64 us (1%)
    pallas_call x1, Pallas kernels, local(): pl.pallas_call(functools.partial(remap_kernel, bands, cols, levels, capac...  50.7 us
    unnamed x2, local copies, waits for them, and re-layouts  3.53 us

profile of v2, /device:TPU:1, one launch (start us, length us, event | category | flops | bytes accessed | tf_op | source)
XLA Modules:
  0.0 54.9 jit_solution(7044202879032147300)
XLA Ops:
  0.6 50.7 %shard_map.104 = (f32[6,16,900]{2,1,0:T(8,128)}, f32[6,16,900]{2,1,0:T(8,128)}) custom-call(s32[2]{0:T(128)} %cutoff.1, s32[256]{0:T(256)} %source_block.1, s32[1,256]{1,0:T(1,128)} %bitcast.2, s32[1,256]{1,0:T(1,128)} %bitcast.3, f32[2,16,512]{2,1,0:T(8,128)} %constant.6.clone.fine, f32[64,2,512]{2,1,0:T(2,128)} %constant.7.clone.coarse, ...), custom_call_target="tpu_custom_call" | custom-call | tf_op jit(solution)/shard_map/pallas_call | solution.py:500
  51.3 1.8 %copy.13 = f32[6,16,900]{2,1,0:T(8,128)} copy(f32[6,16,900]{2,1,0:T(8,128)} %get-tuple-element.4) | data formatting | bytes 691200
  53.1 1.8 %copy.14 = f32[6,16,900]{2,1,0:T(8,128)} copy(f32[6,16,900]{2,1,0:T(8,128)} %get-tuple-element.5) | data formatting | bytes 691200

commit v3 on v2

--- a/solution.py
+++ b/solution.py
@@ -13,8 +13,9 @@
 LANES = 128
 STEP = 16
 CHUNK = 32
-PIECE = 8
-DENSE = (0, 2, 3, 5, 6)
+PIECE = 256
+TOGETHER = 4
+DENSE = (0, 4, 4, 4, 6)
 MESH = pl.DeviceIdType.MESH
 F32 = jnp.float32
 BF16 = jnp.bfloat16
@@ -36,8 +37,8 @@
 
 
 def remap_kernel(
-    bands, cols, levels, capacity, wave_count, period, longitudes, tile_count,
-    cutoff, source_block, owner_row, tile_row, fine, coarse, start, source, weights,
+    bands, cols, width, levels, capacity, wave_count, period, longitudes, tile_count,
+    cutoff, source_block, owner_row, tile_row, fine, coarse, start, turn, source, weights,
     remapped, filtered,
     weight_buf, source_even, source_odd, partial,
     sums, table_high, table_low, rotated, field, slab, recv, relay, relay_sums, passed,
@@ -52,7 +53,16 @@
     rows = levels * capacity
     half_size = cols // 2
     half, place_in_half = col // half_size, lax.rem(col, half_size)
-    counterpart = (band, (1 - half) * half_size + place_in_half)
+    layers = half_size // width
+    layer = place_in_half // width
+
+    def mirror(where):
+        return (layers - 1 - where // width) * width + where % width
+
+    def group_of(where):
+        return jnp.where(half == 0, where, mirror(where))
+
+    counterpart = (band, (1 - half) * half_size + mirror(place_in_half))
 
     def valid(offset):
         target = band + (offset - 1)
@@ -105,10 +115,16 @@
     tags = dot(chosen, tile_at, 1, 1)
     for offset in range(3):
         for to in range(half_size):
-            first = tags[offset * cols + to : offset * cols + to + 1]
-            second = tags[offset * cols + half_size + to : offset * cols + half_size + to + 1]
-            tags_out[offset * half_size + to, 0:1] = jnp.where(half == 0, first, second)
-            tags_out[offset * half_size + to, 1:2] = jnp.where(half == 0, second, first)
+            here = [
+                tags[row : row + 1]
+                for row in (
+                    offset * cols + lat_half * half_size + where
+                    for where in (to, mirror(to))
+                    for lat_half in range(2)
+                )
+            ]
+            tags_out[offset * half_size + to, 0:1] = jnp.where(half == 0, here[0], here[1])
+            tags_out[offset * half_size + to, 1:2] = jnp.where(half == 0, here[3], here[2])
     lat_here = cutoff.shape[0]
     for lat in range(lat_here):
         cut_out[lat : lat + 1] = jnp.full((1, LANES), cutoff[lat], jnp.int32)
@@ -128,6 +144,24 @@
             )
             right = weight_buf[index : index + 2].reshape(2 * LANES, LANES)
             partial[index : index + 2] = dot(left, right).reshape(2, 8, LANES)
+
+    data = jnp.concatenate([partial[:, level, :] for level in range(levels)], axis=1)
+    stacked = jnp.concatenate(split(data), axis=0)
+
+    def fill(offset):
+        group = cols * capacity
+        ids = lax.broadcasted_iota(jnp.int32, (group, blocks), 0) + offset * group
+        placing = (ids == slot).astype(F32).astype(BF16)
+        placed = dot(jnp.concatenate([placing, placing], axis=1), stacked)
+        here = pl.ds(offset * cols, cols)
+        for level in range(levels):
+            piece = placed[:, level * LANES : (level + 1) * LANES]
+            slab[here, level * capacity : (level + 1) * capacity, :] = piece.reshape(
+                cols, capacity, LANES
+            )
+
+    pl.when(valid(0))(functools.partial(fill, 0))
+    pl.when(band == 0)(functools.partial(fill, 2))
 
     inner_band = (band > 0) & (band < bands - 1)
     neighbours = jnp.where(inner_band, 2, 1) if bands > 1 else 0
@@ -164,9 +198,9 @@
             tag_send, tag_recv, offset,
         )
 
-    def push(owner_half, into, sems, offset):
+    def push(owner_half, owner_of, into, sems, offset):
         send_to_half(
-            lambda to: slab.at[offset * cols + owner_half * half_size + to],
+            lambda to: slab.at[offset * cols + owner_half * half_size + owner_of(to)],
             into.at[(2 - offset) * half_size + place_in_half],
             send_sem, sems, offset,
         )
@@ -183,35 +217,22 @@
         pl.when(valid(offset))(functools.partial(push_tags, offset))
     cut_copy.start()
 
-    data = jnp.concatenate([partial[:, level, :] for level in range(levels)], axis=1)
-    stacked = jnp.concatenate(split(data), axis=0)
-
-    def fill(offset):
-        group = cols * capacity
-        ids = lax.broadcasted_iota(jnp.int32, (group, blocks), 0) + offset * group
-        placing = (ids == slot).astype(F32).astype(BF16)
-        placed = dot(jnp.concatenate([placing, placing], axis=1), stacked)
-        here = pl.ds(offset * cols, cols)
-        for level in range(levels):
-            piece = placed[:, level * LANES : (level + 1) * LANES]
-            slab[here, level * capacity : (level + 1) * capacity, :] = piece.reshape(
-                cols, capacity, LANES
-            )
-
     def place_and_push(offset):
-        fill(offset)
-        push(1 - half, relay, relay_sem, offset)
+        if offset == 1:
+            fill(offset)
+        elif offset == 2:
+            pl.when(band > 0)(functools.partial(fill, offset))
+        push(1 - half, mirror, relay, relay_sem, offset)
 
     for offset in (0, 2, 1):
         pl.when(valid(offset))(functools.partial(place_and_push, offset))
     for offset in (0, 2, 1):
-        pl.when(valid(offset))(functools.partial(push, half, recv, recv_sem, offset))
+        pl.when(valid(offset))(functools.partial(push, half, lambda to: to, recv, recv_sem, offset))
 
     begin = start[col]
     cos_start, sin_start = begin[0:1], begin[1:2]
     rotated[0] = fine[0] * cos_start - fine[1] * sin_start
     rotated[1] = fine[1] * cos_start + fine[0] * sin_start
-    parity = wave_count // 2
 
     def table_step(step, carry):
         pair = coarse[step]
@@ -220,14 +241,11 @@
         at = pl.ds(pl.multiple_of(step * STEP, STEP), STEP)
         for first, value in (
             (0, cos_base * cos_fine - sin_base * sin_fine),
-            (parity, sin_base * cos_fine + cos_base * sin_fine),
+            (wave_count, sin_base * cos_fine + cos_base * sin_fine),
         ):
             high, low = split(value)
-            for odd in range(2):
-                here = slice(first + odd * wave_count, first + odd * wave_count + parity)
-                there = slice(odd * parity, (odd + 1) * parity)
-                table_high[at, here] = high[:, there]
-                table_low[at, here] = low[:, there]
+            table_high[at, first : first + wave_count] = high
+            table_low[at, first : first + wave_count] = low
         return carry
 
     lax.fori_loop(0, coarse.shape[0], table_step, 0)
@@ -284,17 +302,20 @@
             device_id_type=MESH,
         ).start()
 
+    inner = jnp.where(half == 0, layer >= layers // 2, layer < layers - layers // 2)
+    outer = jnp.logical_not(inner)
     ends = [levels * share // DENSE[-1] for share in DENSE]
 
     def dense_part(index):
         if ends[index + 1] > ends[index]:
-            dense_start(ends[index], ends[index + 1] - ends[index])
+            pl.when(outer)(
+                functools.partial(dense_start, ends[index], ends[index + 1] - ends[index])
+            )
 
     for offset in (0, 2, 1):
         pl.when(valid(offset))(functools.partial(receive, relay, relay_sem, relay_sums, 1, offset))
+    pl.when(inner)(functools.partial(dense_start, 0, levels))
     dense_part(0)
-    for offset in (0, 2, 1):
-        pl.when(valid(offset))(functools.partial(receive, recv, recv_sem, sums, 0, offset))
 
     long_tiles, field_rows = field.shape[1:3]
     lat_band = field_rows // levels
@@ -306,7 +327,8 @@
     def row_of(level, lat):
         owner, within = divmod(lat, lat_here)
         lat_half, owner_place = divmod(owner, half_size)
-        return owner_place * group_rows + (level * 2 + lat_half) * lat_here + within
+        group = mirror(owner_place) if lat_half else owner_place
+        return group * group_rows + (level * 2 + lat_half) * lat_here + within
 
     def lat_rows(ref, lat):
         first, shift = divmod(lat * longitudes, LANES)
@@ -320,22 +342,31 @@
             )
         return jnp.where(inside, value, 0.0)
 
-    for lat in range(lat_band):
-        own, relayed = lat_rows(sums, lat), lat_rows(relay_sums, lat)
-        both, apart = own + relayed, own - relayed
-        for level in range(levels):
-            field[0, :, row_of(level, lat), :] = both[level]
-            field[1, :, row_of(level, lat), :] = apart[level]
-
-    for odd in range(2):
-        rows_wide = jnp.concatenate([field[odd, tile] for tile in range(long_tiles)], axis=1)
+    def rows_of_field(ref, index):
+        for lat in range(lat_band):
+            value = lat_rows(ref, lat)
+            for level in range(levels):
+                field[index, :, row_of(level, lat), :] = value[level]
+        rows_wide = jnp.concatenate([field[index, tile] for tile in range(long_tiles)], axis=1)
         high, low = split(rows_wide)
-        waves = slice(odd * wave_count, (odd + 1) * wave_count)
-        both = dot(jnp.concatenate([high, low], axis=0), table_high[:, waves])
-        spectrum = both[:field_rows] + both[field_rows:] + dot(high, table_low[:, waves])
-        spectra[:, :, waves] = spectrum.reshape(half_size, group_rows, wave_count)
-
-    pieces = [pl.ds(first, PIECE) for first in range(0, group_rows, PIECE)]
+        return jnp.concatenate([high, low], axis=0), high
+
+    def transformed(parts, waves):
+        both = dot(parts[0], table_high[:, waves])
+        return both[:field_rows] + both[field_rows:] + dot(parts[1], table_low[:, waves])
+
+    relayed = transformed(rows_of_field(relay_sums, 1), slice(None))
+    angle = turn[col]
+    cos_part, sin_part = relayed[:, :wave_count], relayed[:, wave_count:]
+    grouped = (half_size, group_rows, wave_count)
+    spectra[:, :, :wave_count] = (cos_part * angle[0:1] - sin_part * angle[1:2]).reshape(grouped)
+    spectra[:, :, wave_count:] = (sin_part * angle[0:1] + cos_part * angle[1:2]).reshape(grouped)
+
+    for offset in (0, 2, 1):
+        pl.when(valid(offset))(functools.partial(receive, recv, recv_sem, sums, 0, offset))
+
+    waves = 2 * wave_count
+    pieces = [slice(first, first + PIECE) for first in range(0, waves, PIECE)]
 
     def to_half(source_of, target, sem_out, sem_in):
         def one(step, carry):
@@ -357,10 +388,16 @@
         lax.fori_loop(0, half_size, one, 0)
         pltpu.make_async_copy(source_of(place_in_half), target, sem_in).start()
 
+    parts = rows_of_field(sums, 0)
     for i, piece in enumerate(pieces):
+        if i % TOGETHER == 0:
+            wide = slice(piece.start, piece.start + TOGETHER * PIECE)
+            spectra[:, :, wide] += transformed(parts, wide).reshape(
+                half_size, group_rows, TOGETHER * PIECE
+            )
         to_half(
-            lambda to: spectra.at[to, piece],
-            arrived.at[place_in_half, piece],
+            lambda to: spectra.at[group_of(to), :, piece],
+            arrived.at[place_in_half, :, piece],
             scatter_send.at[i], scatter_recv.at[i],
         )
     dense_part(1)
@@ -372,22 +409,20 @@
             cuts.append(
                 jnp.where(half == lat_half, cut_out[lat : lat + 1], cut_in[lat : lat + 1])
             )
-    cut_rows = jnp.concatenate(cuts * (PIECE // len(cuts)), axis=0)
+    cut_rows = jnp.concatenate(cuts * (group_rows // len(cuts)), axis=0)
 
     def gain_of(tile):
-        j = lax.broadcasted_iota(jnp.int32, (PIECE, LANES), 1) + tile * LANES
-        odd, within = j // wave_count, lax.rem(j, wave_count)
-        wave = 2 * lax.rem(within, parity) + odd
+        j = lax.broadcasted_iota(jnp.int32, (group_rows, LANES), 1) + tile * LANES
+        wave = jnp.where(j >= wave_count, j - wave_count, j)
         weight = jnp.where(wave == 0, 1.0, 2.0) / period
         return jnp.where(wave <= cut_rows, weight, 0.0).astype(F32)
 
-    wave_tiles = spectra.shape[2] // LANES
-    gains = jnp.concatenate([gain_of(tile) for tile in range(wave_tiles)], axis=1)
+    gains = jnp.concatenate([gain_of(tile) for tile in range(waves // LANES)], axis=1)
 
     def cross(i):
         return pltpu.make_async_remote_copy(
-            src_ref=half_sum.at[pieces[i]],
-            dst_ref=other_sum.at[pieces[i]],
+            src_ref=half_sum.at[:, pieces[i]],
+            dst_ref=other_sum.at[:, pieces[i]],
             send_sem=cross_send.at[i],
             recv_sem=cross_recv.at[i],
             device_id=counterpart,
@@ -395,20 +430,20 @@
         )
 
     for i, piece in enumerate(pieces):
-        here = arrived.at[:, piece]
+        here = arrived.at[:, :, piece]
         pltpu.make_async_copy(here, here, scatter_recv.at[i]).wait()
-        total = arrived[0, piece]
+        total = arrived[0, :, piece]
         for sender in range(1, half_size):
-            total += arrived[sender, piece]
-        half_sum[piece] = total
+            total += arrived[sender, :, piece]
+        half_sum[:, piece] = total
         cross(i).start()
     dense_part(2)
     for i, piece in enumerate(pieces):
         cross(i).wait_recv()
-        scaled[piece] = (half_sum[piece] + other_sum[piece]) * gains
+        scaled[:, piece] = (half_sum[:, piece] + other_sum[:, piece]) * gains[:, piece]
         to_half(
-            lambda to: scaled.at[piece],
-            gathered.at[place_in_half, piece],
+            lambda to: scaled.at[:, piece],
+            gathered.at[group_of(place_in_half), :, piece],
             spread_send.at[i], spread_recv.at[i],
         )
     dense_part(3)
@@ -422,7 +457,7 @@
     for offset in range(3):
         pl.when(valid(offset))(functools.partial(drain, offset))
     for i, piece in enumerate(pieces):
-        others = arrived.at[pl.ds(0, half_size - 1), piece]
+        others = arrived.at[pl.ds(0, half_size - 1), :, piece]
         pltpu.make_async_copy(others, others, scatter_send.at[i]).wait()
         cross(i).wait_send()
 
@@ -436,13 +471,14 @@
             levels, lat_band, longitudes
         )
 
+    result = None
     for i, piece in enumerate(pieces):
-        here = gathered.at[:, piece]
+        here = gathered.at[:, :, piece]
         pltpu.make_async_copy(here, here, spread_recv.at[i]).wait()
-    spectrum = gathered[...].reshape(field_rows, 2 * wave_count)
-    high, low = split(spectrum)
-    both = dot(jnp.concatenate([high, low], axis=0), table_high[...], 1, 1)
-    result = both[:field_rows] + both[field_rows:] + dot(high, table_low[...], 1, 1)
+        high, low = split(gathered[:, :, piece].reshape(field_rows, PIECE))
+        both = dot(jnp.concatenate([high, low], axis=0), table_high[:, piece], 1, 1)
+        added = both[:field_rows] + both[field_rows:] + dot(high, table_low[:, piece], 1, 1)
+        result = added if result is None else result + added
     filtered[...] = natural(result)
 
     pltpu.make_async_copy(passed, passed, pass_recv).wait()
@@ -456,15 +492,34 @@
 
     pltpu.make_async_copy(passed, passed, pass_send).wait()
     for i, piece in enumerate(pieces):
-        others = arrived.at[pl.ds(0, half_size - 1), piece]
+        others = arrived.at[pl.ds(0, half_size - 1), :, piece]
         pltpu.make_async_copy(others, others, spread_send.at[i]).wait()
 
 
+def deliver(first, second, first_out, second_out, sem):
+    copies = [
+        pltpu.make_async_copy(first, first_out, sem.at[0]),
+        pltpu.make_async_copy(second, second_out, sem.at[1]),
+    ]
+    for copy in copies:
+        copy.start()
+    for copy in copies:
+        copy.wait()
+
+
 def cos_sin(positions):
-    waves = np.concatenate([np.arange(0, KW, 2), np.arange(1, KW, 2)])
-    phases = positions[:, None] * waves[None, :] % NLON
+    phases = positions[:, None] * np.arange(KW)[None, :] % NLON
     angles = phases * (2 * np.pi / NLON)
     return np.cos(angles).astype(np.float32), np.sin(angles).astype(np.float32)
+
+
+def width_of(mesh):
+    cols = mesh.shape["col"]
+    places = [getattr(device, "coords", None) for device in mesh.devices[0]]
+    if None in places:
+        return 1
+    width = sum(place[2] == places[0][2] for place in places)
+    return width if cols % (2 * width) == 0 else 1
 
 
 def local(mesh, source, weights, source_block, owner_device, target_tile, cutoff):
@@ -483,13 +538,18 @@
     long_pad = round_up(longitudes, LANES)
     long_tiles = long_pad // LANES
     tiles = round_up(tile_count + long_tiles, LANES)
-    sent_tiles = round_up(tile_count, 8)
+    sent_tiles = tile_count
     group_rows = levels * lat_band // half_size
-    pieces = group_rows // PIECE
+    pieces = 2 * KW // PIECE
     chunks = block_count // CHUNK
     fine = np.stack(cos_sin(np.arange(STEP)))
     coarse = np.stack(cos_sin(STEP * np.arange(long_pad // STEP)), axis=1)
     start = np.stack(cos_sin(longitudes * np.arange(cols)), axis=1)
+    width = width_of(mesh)
+    places = np.arange(half_size)
+    mirrored = (half_size // width - 1 - places // width) * width + places % width
+    away = np.concatenate([half_size + mirrored - places, mirrored - places - half_size])
+    turn = np.stack(cos_sin(longitudes * away % NLON), axis=1)
 
     slab_rows = levels * capacity
     smem = pl.BlockSpec(memory_space=pltpu.SMEM)
@@ -497,12 +557,12 @@
     anywhere = pl.BlockSpec(memory_space=pl.ANY)
     shape = jax.ShapeDtypeStruct((levels, lat_band, longitudes), F32)
     dma = pltpu.SemaphoreType.DMA
-    return pl.pallas_call(
+    results = pl.pallas_call(
         functools.partial(
-            remap_kernel, bands, cols, levels, capacity, KW, NLON, longitudes, sent_tiles
+            remap_kernel, bands, cols, width, levels, capacity, KW, NLON, longitudes, sent_tiles
         ),
-        out_shape=(shape, shape),
-        in_specs=[smem] * 2 + [vmem] * 6 + [anywhere],
+        out_shape=(pltpu.VMEM(shape.shape, F32), pltpu.VMEM(shape.shape, F32)),
+        in_specs=[smem] * 2 + [vmem] * 7 + [anywhere],
         out_specs=(vmem, vmem),
         scratch_shapes=[
             pltpu.VMEM(weights.shape, BF16),
@@ -547,19 +607,32 @@
             dma((pieces,)),
         ],
         compiler_params=pltpu.CompilerParams(
-            collective_id=0, has_side_effects=True, vmem_limit_bytes=56 << 20
+            collective_id=0, has_side_effects=True, vmem_limit_bytes=48 << 20
         ),
     )(
-        cutoff,
-        source_block,
-        owner_device.reshape(1, block_count),
-        target_tile.reshape(1, block_count),
-        fine,
-        coarse,
-        start,
-        source,
-        weights,
+        *(
+            pltpu.with_memory_space_constraint(operand, pltpu.HBM)
+            for operand in (
+                cutoff,
+                source_block,
+                owner_device.reshape(1, block_count),
+                target_tile.reshape(1, block_count),
+                jnp.asarray(fine),
+                jnp.asarray(coarse),
+                jnp.asarray(start),
+                jnp.asarray(turn),
+                source,
+                weights,
+            )
+        )
     )
+    return pl.pallas_call(
+        deliver,
+        out_shape=(shape, shape),
+        in_specs=[vmem] * 2,
+        out_specs=(anywhere, anywhere),
+        scratch_shapes=[dma((2,))],
+    )(*(pltpu.with_memory_space_constraint(result, pltpu.VMEM) for result in results))
 
 
 def solution(mesh):

time: 55.1 us -> 48.3 us (0.88)
  local copies, waits for them, and re-layouts: 3.53 us -> 0 us
  Pallas kernels: 50.7 us -> 47.5 us
    unnamed x2 -> x0, local copies, waits for them, and re-layouts: 3.53 us -> none
    pallas_call x1 -> x2, Pallas kernels: 50.7 us -> 47.5 us  [the longest x1 46.6 us: local(): pl.pallas_call(functools.partial(remap_kernel, bands, cols, width, levels...]
where the time goes in v3:
time: 48.3 us; the launch traced here: 48.1 us
  Pallas kernels  47.5 us (98%)
  between operations  0.64 us (1%)
    pallas_call x1, Pallas kernels, local(): pl.pallas_call(functools.partial(remap_kernel, bands, cols, width, levels...  46.6 us

profile of v3, /device:TPU:1, one launch (start us, length us, event | category | flops | bytes accessed | tf_op | source)
XLA Modules:
  0.0 48.1 jit_solution(14058869939155756749)
XLA Ops:
  0.6 46.6 %shard_map.113 = (f32[6,16,900]{2,1,0:T(8,128)S(1)}, f32[6,16,900]{2,1,0:T(8,128)S(1)}) custom-call(s32[2]{0:T(128)} %cutoff.1, s32[256]{0:T(256)} %source_block.1, s32[1,256]{1,0:T(1,128)} %bitcast.2, s32[1,256]{1,0:T(1,128)} %bitcast.3, f32[2,16,512]{2,1,0:T(8,128)} %constant.8.clone.fine, f32[64,2,512]{2,1,0:T(2,128)} %constant.9.clone.coarse, ...), custom_call_target="tpu_custom_call" | custom-call | tf_op jit(solution)/shard_map/pallas_call | solution.py:560
  47.2 0.9 %shard_map.114 = (f32[6,16,900]{2,1,0:T(8,128)}, f32[6,16,900]{2,1,0:T(8,128)}) custom-call(f32[6,16,900]{2,1,0:T(8,128)S(1)} %get-tuple-element.4.first, f32[6,16,900]{2,1,0:T(8,128)S(1)} %get-tuple-element.5.second), custom_call_target="tpu_custom_call" | custom-call | tf_op jit(solution)/shard_map/pallas_call | solution.py:629

commit v4 on v3

--- a/solution.py
+++ b/solution.py
@@ -15,7 +15,9 @@
 CHUNK = 32
 PIECE = 256
 TOGETHER = 4
-DENSE = (0, 4, 4, 4, 6)
+EARLY = 2
+BETWEEN = 1
+DENSE = (0, 4, 4, 4, 5, 6)
 MESH = pl.DeviceIdType.MESH
 F32 = jnp.float32
 BF16 = jnp.bfloat16
@@ -38,15 +40,16 @@
 
 def remap_kernel(
     bands, cols, width, levels, capacity, wave_count, period, longitudes, tile_count,
-    cutoff, source_block, owner_row, tile_row, fine, coarse, start, turn, source, weights,
+    cutoff_in, block_in, owner_in, tile_in, source_in, fine_in, coarse_in, start_in, turn_in, weights,
     remapped, filtered,
+    cutoff, source_block, owner_row, tile_row, source, fine, coarse, start, turn,
     weight_buf, source_even, source_odd, partial,
     sums, table_high, table_low, rotated, field, slab, recv, relay, relay_sums, passed,
     tags_out, tags_in, cut_out, cut_in,
     spectra, arrived, half_sum, other_sum, scaled, gathered,
     weight_sem, tag_send, tag_recv, cut_send, cut_recv,
     send_sem, recv_sem, relay_sem, pass_send, pass_recv,
-    scatter_send, scatter_recv, cross_send, cross_recv, spread_send, spread_recv,
+    scatter_send, scatter_recv, cross_send, cross_recv, spread_send, spread_recv, operand_sem,
 ):
     band, col = lax.axis_index("band"), lax.axis_index("col")
     blocks = weights.shape[0]
@@ -74,7 +77,23 @@
         )
         for i, first in enumerate(range(0, blocks, CHUNK))
     ]
-    for copy in weight_copies:
+    operand_copies = [
+        pltpu.make_async_copy(there, here, operand_sem.at[i])
+        for i, (there, here) in enumerate(
+            (
+                (owner_in, owner_row),
+                (tile_in, tile_row),
+                (block_in, source_block),
+                (source_in, source),
+                (cutoff_in, cutoff),
+                (fine_in, fine),
+                (coarse_in, coarse),
+                (start_in, start),
+                (turn_in, turn),
+            )
+        )
+    ]
+    for copy in operand_copies[:5] + weight_copies[:EARLY]:
         copy.start()
 
     barrier = pltpu.get_barrier_semaphore()
@@ -93,12 +112,16 @@
                 signal()
             return carry
 
-        lax.fori_loop(0, half_size, one, 0)
+        lax.fori_loop(0, half_size, one, 0, unroll=half_size <= 4)
 
     for offset in (0, 2, 1):
         pl.when(valid(offset))(functools.partial(greet_half, offset))
     greet(counterpart)
 
+    for copy in operand_copies[:3]:
+        copy.wait()
+    for copy in weight_copies[EARLY:] + operand_copies[5:]:
+        copy.start()
     owners = owner_row[...]
     sublane = lax.broadcasted_iota(jnp.int32, (blocks, blocks), 0)
     lane = lax.broadcasted_iota(jnp.int32, (blocks, blocks), 1)
@@ -126,6 +149,8 @@
             tags_out[offset * half_size + to, 0:1] = jnp.where(half == 0, here[0], here[1])
             tags_out[offset * half_size + to, 1:2] = jnp.where(half == 0, here[3], here[2])
     lat_here = cutoff.shape[0]
+    for copy in operand_copies[3:5]:
+        copy.wait()
     for lat in range(lat_here):
         cut_out[lat : lat + 1] = jnp.full((1, LANES), cutoff[lat], jnp.int32)
 
@@ -187,7 +212,7 @@
                 start_remote()
             return carry
 
-        lax.fori_loop(0, half_size, one, 0)
+        lax.fori_loop(0, half_size, one, 0, unroll=half_size <= 4)
         if offset == 1:
             pltpu.make_async_copy(source_of(place_in_half), target, sems_in.at[1]).start()
 
@@ -213,9 +238,6 @@
         device_id=counterpart,
         device_id_type=MESH,
     )
-    for offset in (0, 2, 1):
-        pl.when(valid(offset))(functools.partial(push_tags, offset))
-    cut_copy.start()
 
     def place_and_push(offset):
         if offset == 1:
@@ -224,11 +246,18 @@
             pl.when(band > 0)(functools.partial(fill, offset))
         push(1 - half, mirror, relay, relay_sem, offset)
 
+    pl.when(valid(0))(functools.partial(place_and_push, 0))
+    pl.when(band == 0)(functools.partial(place_and_push, 2))
     for offset in (0, 2, 1):
-        pl.when(valid(offset))(functools.partial(place_and_push, offset))
+        pl.when(valid(offset))(functools.partial(push_tags, offset))
+    cut_copy.start()
+    pl.when((band > 0) & valid(2))(functools.partial(place_and_push, 2))
+    place_and_push(1)
     for offset in (0, 2, 1):
         pl.when(valid(offset))(functools.partial(push, half, lambda to: to, recv, recv_sem, offset))
 
+    for copy in operand_copies[5:]:
+        copy.wait()
     begin = start[col]
     cos_start, sin_start = begin[0:1], begin[1:2]
     rotated[0] = fine[0] * cos_start - fine[1] * sin_start
@@ -385,7 +414,7 @@
             pl.when(to != place_in_half)(start_remote)
             return carry
 
-        lax.fori_loop(0, half_size, one, 0)
+        lax.fori_loop(0, half_size, one, 0, unroll=half_size <= 4)
         pltpu.make_async_copy(source_of(place_in_half), target, sem_in).start()
 
     parts = rows_of_field(sums, 0)
@@ -446,7 +475,9 @@
             gathered.at[group_of(place_in_half), :, piece],
             spread_send.at[i], spread_recv.at[i],
         )
-    dense_part(3)
+        if i == BETWEEN:
+            dense_part(3)
+    dense_part(4)
 
     def drain(offset):
         sent = slab.at[pl.ds(0, cols - 2 if offset == 1 else cols)]
@@ -552,7 +583,6 @@
     turn = np.stack(cos_sin(longitudes * away % NLON), axis=1)
 
     slab_rows = levels * capacity
-    smem = pl.BlockSpec(memory_space=pltpu.SMEM)
     vmem = pl.BlockSpec(memory_space=pltpu.VMEM)
     anywhere = pl.BlockSpec(memory_space=pl.ANY)
     shape = jax.ShapeDtypeStruct((levels, lat_band, longitudes), F32)
@@ -562,9 +592,18 @@
             remap_kernel, bands, cols, width, levels, capacity, KW, NLON, longitudes, sent_tiles
         ),
         out_shape=(pltpu.VMEM(shape.shape, F32), pltpu.VMEM(shape.shape, F32)),
-        in_specs=[smem] * 2 + [vmem] * 7 + [anywhere],
+        in_specs=[anywhere] * 10,
         out_specs=(vmem, vmem),
         scratch_shapes=[
+            pltpu.SMEM(cutoff.shape, jnp.int32),
+            pltpu.SMEM(source_block.shape, jnp.int32),
+            pltpu.VMEM((1, block_count), jnp.int32),
+            pltpu.VMEM((1, block_count), jnp.int32),
+            pltpu.VMEM(source.shape, BF16),
+            pltpu.VMEM(fine.shape, F32),
+            pltpu.VMEM(coarse.shape, F32),
+            pltpu.VMEM(start.shape, F32),
+            pltpu.VMEM(turn.shape, F32),
             pltpu.VMEM(weights.shape, BF16),
             pltpu.VMEM((source.shape[1] // LANES, 16, LANES), BF16),
             pltpu.VMEM((source.shape[1] // LANES, 16, LANES), BF16),
@@ -605,6 +644,7 @@
             dma((pieces,)),
             dma((pieces,)),
             dma((pieces,)),
+            dma((9,)),
         ],
         compiler_params=pltpu.CompilerParams(
             collective_id=0, has_side_effects=True, vmem_limit_bytes=48 << 20
@@ -617,11 +657,11 @@
                 source_block,
                 owner_device.reshape(1, block_count),
                 target_tile.reshape(1, block_count),
+                source,
                 jnp.asarray(fine),
                 jnp.asarray(coarse),
                 jnp.asarray(start),
                 jnp.asarray(turn),
-                source,
                 weights,
             )
         )

time: 48.3 us -> 47.7 us (0.988)
  Pallas kernels: 47.5 us -> 46.9 us
    pallas_call x1, Pallas kernels: 46.6 us -> 46 us  [local(): pl.pallas_call(functools.partial(remap_kernel, bands, cols, width, levels...]
where the time goes in v4:
time: 47.7 us; the launch traced here: 47.5 us
  Pallas kernels  46.9 us (98%)
  between operations  0.64 us (1%)
    pallas_call x1, Pallas kernels, local(): pl.pallas_call(functools.partial(remap_kernel, bands, cols, width, levels...  46 us

profile of v4, /device:TPU:1, one launch (start us, length us, event | category | flops | bytes accessed | tf_op | source)
XLA Modules:
  0.0 47.5 jit_solution(7246391201450113710)
XLA Ops:
  0.6 46.0 %shard_map.113 = (f32[6,16,900]{2,1,0:T(8,128)S(1)}, f32[6,16,900]{2,1,0:T(8,128)S(1)}) custom-call(s32[2]{0:T(128)} %cutoff_in.1, s32[256]{0:T(256)} %block_in.1, s32[1,256]{1,0:T(1,128)} %bitcast.2, s32[1,256]{1,0:T(1,128)} %bitcast.3, bf16[6,16384]{1,0:T(8,128)(2,1)} %source_in.1, f32[2,16,512]{2,1,0:T(8,128)} %constant.8.clone.fine_in, ...), custom_call_target="tpu_custom_call" | custom-call | tf_op jit(solution)/shard_map/pallas_call | solution.py:590
  46.6 0.9 %shard_map.114 = (f32[6,16,900]{2,1,0:T(8,128)}, f32[6,16,900]{2,1,0:T(8,128)}) custom-call(f32[6,16,900]{2,1,0:T(8,128)S(1)} %get-tuple-element.4.first, f32[6,16,900]{2,1,0:T(8,128)S(1)} %get-tuple-element.5.second), custom_call_target="tpu_custom_call" | custom-call | tf_op jit(solution)/shard_map/pallas_call | solution.py:669

commit v5 on v4

--- a/solution.py
+++ b/solution.py
@@ -43,7 +43,7 @@
     cutoff_in, block_in, owner_in, tile_in, source_in, fine_in, coarse_in, start_in, turn_in, weights,
     remapped, filtered,
     cutoff, source_block, owner_row, tile_row, source, fine, coarse, start, turn,
-    weight_buf, source_even, source_odd, partial,
+    weight_buf, source_even, source_odd, partial, stacked,
     sums, table_high, table_low, rotated, field, slab, recv, relay, relay_sums, passed,
     tags_out, tags_in, cut_out, cut_in,
     spectra, arrived, half_sum, other_sum, scaled, gathered,
@@ -161,8 +161,18 @@
         source_even[index] = jnp.concatenate([value, above], axis=0)
         source_odd[index] = jnp.concatenate([below, value, above[: 8 - levels]], axis=0)
 
+    def pack(i):
+        here = slice(i * CHUNK, (i + 1) * CHUNK)
+        for level in range(levels):
+            high, low = split(partial[here, level, :])
+            columns = slice(level * LANES, (level + 1) * LANES)
+            stacked[here, columns] = high
+            stacked[blocks + here.start : blocks + here.stop, columns] = low
+
     for i, copy in enumerate(weight_copies):
         copy.wait()
+        if i:
+            pack(i - 1)
         for index in range(i * CHUNK, (i + 1) * CHUNK, 2):
             left = jnp.concatenate(
                 [source_even[source_block[index]], source_odd[source_block[index + 1]]], axis=1
@@ -170,14 +180,13 @@
             right = weight_buf[index : index + 2].reshape(2 * LANES, LANES)
             partial[index : index + 2] = dot(left, right).reshape(2, 8, LANES)
 
-    data = jnp.concatenate([partial[:, level, :] for level in range(levels)], axis=1)
-    stacked = jnp.concatenate(split(data), axis=0)
+    pack(len(weight_copies) - 1)
 
     def fill(offset):
         group = cols * capacity
         ids = lax.broadcasted_iota(jnp.int32, (group, blocks), 0) + offset * group
         placing = (ids == slot).astype(F32).astype(BF16)
-        placed = dot(jnp.concatenate([placing, placing], axis=1), stacked)
+        placed = dot(jnp.concatenate([placing, placing], axis=1), stacked[...])
         here = pl.ds(offset * cols, cols)
         for level in range(levels):
             piece = placed[:, level * LANES : (level + 1) * LANES]
@@ -608,6 +617,7 @@
             pltpu.VMEM((source.shape[1] // LANES, 16, LANES), BF16),
             pltpu.VMEM((source.shape[1] // LANES, 16, LANES), BF16),
             pltpu.VMEM((block_count, 8, LANES), F32),
+            pltpu.VMEM((2 * block_count, levels * LANES), BF16),
             pltpu.VMEM((levels, tiles, LANES), F32),
             pltpu.VMEM((long_pad, 2 * KW), BF16),
             pltpu.VMEM((long_pad, 2 * KW), BF16),

time: 47.7 us -> 47.6 us (level)
  no operation moved by 1% of the time
where the time goes in v5:
time: 47.6 us; the launch traced here: 47.5 us
  Pallas kernels  46.8 us (98%)
  between operations  0.64 us (1%)
    pallas_call x1, Pallas kernels, local(): pl.pallas_call(functools.partial(remap_kernel, bands, cols, width, levels...  45.9 us

profile of v5, /device:TPU:1, one launch (start us, length us, event | category | flops | bytes accessed | tf_op | source)
XLA Modules:
  0.0 47.5 jit_solution(4775807210411895722)
XLA Ops:
  0.6 45.9 %shard_map.113 = (f32[6,16,900]{2,1,0:T(8,128)S(1)}, f32[6,16,900]{2,1,0:T(8,128)S(1)}) custom-call(s32[2]{0:T(128)} %cutoff_in.1, s32[256]{0:T(256)} %block_in.1, s32[1,256]{1,0:T(1,128)} %bitcast.2, s32[1,256]{1,0:T(1,128)} %bitcast.3, bf16[6,16384]{1,0:T(8,128)(2,1)} %source_in.1, f32[2,16,512]{2,1,0:T(8,128)} %constant.8.clone.fine_in, ...), custom_call_target="tpu_custom_call" | custom-call | tf_op jit(solution)/shard_map/pallas_call | solution.py:599
  46.6 0.9 %shard_map.114 = (f32[6,16,900]{2,1,0:T(8,128)}, f32[6,16,900]{2,1,0:T(8,128)}) custom-call(f32[6,16,900]{2,1,0:T(8,128)S(1)} %get-tuple-element.4.first, f32[6,16,900]{2,1,0:T(8,128)S(1)} %get-tuple-element.5.second), custom_call_target="tpu_custom_call" | custom-call | tf_op jit(solution)/shard_map/pallas_call | solution.py:679
